TPU v7x, 32 devices: a whole 2x2x4 slice. The times are simulated.
32 devices in a mesh: seq: 8 (over z, x), tensor: 4 (over y, core).
Axes of the slice: x: 2, y: 2, z: 4, core: 2. Of those that a mesh axis runs over, the one named last changes fastest.
Arguments:
- tokens: bfloat16 [4096, 2048], P('seq', 'tensor'), may hold values from -12 to 12
- attn_gain: float32 [2048], replicated, may hold values from 0.1 to 1.9
- w_query: bfloat16 [2048, 2048], P('seq', 'tensor'), as said below
- w_key: bfloat16 [2048, 512], P('seq', 'tensor'), as said below
- w_value: bfloat16 [2048, 512], P('seq', 'tensor'), may hold values from -0.125 to 0.125
- w_out: bfloat16 [2048, 2048], P('tensor', 'seq'), may hold values from -0.125 to 0.125
- mlp_gain: float32 [2048], replicated, may hold values from 0.1 to 1.9
- w_gate: bfloat16 [2048, 5632], P('seq', 'tensor'), may hold values from -0.125 to 0.125
- w_up: bfloat16 [2048, 5632], P('seq', 'tensor'), may hold values from -0.125 to 0.125
- w_down: bfloat16 [5632, 2048], P('tensor', 'seq'), may hold values from -0.078125 to 0.078125
Outputs:
- layer_out: bfloat16 [4096, 2048], P('seq', 'tensor')
Inputs may be any that keep to these rules, and one draw needn't show every extreme that they name: `w_query`: entries are of order 2048 to the power -1/2. `w_key`: entries are of order 2048 to the power -1/2.
All inputs are finite; a program needn't handle non-finite values.
Results may differ from a plain program's by a relative error of at most 0.013.
Values may be sent and summed in bfloat16 or wider, within the bound.
A program may use at most 128 MiB of HBM per device.

v0:
```python
import jax
import jax.numpy as jnp
from jax import lax
from jax.sharding import PartitionSpec as P

HEAD_DIM = 128
WINDOW = 1024


def passed_along(block, axis, distance):
    devices = range(lax.axis_size(axis))
    route = [(i - distance, i) for i in devices if i - distance in devices]
    return lax.ppermute(block, axis, route)


def scaled_rows(values, gain):
    values = values.astype(jnp.float32)
    mean_square = jnp.mean(values * values, axis=1, keepdims=True)
    return (values * lax.rsqrt(mean_square + 1e-06) * gain).astype(jnp.bfloat16)


def product(left, right):
    return jnp.dot(left, right, preferred_element_type=jnp.float32)


def window_attention(queries, context_keys, context_values, reach, position):
    rows = queries.shape[0]
    local_kv = context_keys.shape[1] // HEAD_DIM
    group = queries.shape[1] // (local_kv * HEAD_DIM)
    block = min(512, rows)
    span = WINDOW + block
    scale = HEAD_DIM ** (-0.5)
    start = reach * rows - WINDOW
    query_block = queries.reshape(block, local_kv, group, HEAD_DIM)
    key_block = context_keys.reshape(span, local_kv, HEAD_DIM)
    value_block = context_values.reshape(span, local_kv, HEAD_DIM)
    scores = (
        jnp.einsum("qkgd,ckd->kgqc", query_block, key_block, preferred_element_type=jnp.float32)
        * scale
    )
    query_pos = lax.broadcasted_iota(jnp.int32, (block, span), 0)
    key_pos = lax.broadcasted_iota(jnp.int32, (block, span), 1)
    distance = query_pos + WINDOW - key_pos
    first_key = (position - reach) * rows + start
    allowed = (distance >= 0) & (distance < WINDOW) & (key_pos + first_key >= 0)
    scores = jnp.where(allowed[None, None], scores, -1e30)
    highest = jnp.max(scores, axis=3, keepdims=True)
    raised = jnp.exp(scores - highest)
    weights = (raised / jnp.sum(raised, axis=3, keepdims=True)).astype(jnp.bfloat16)
    mixed = jnp.einsum("kgqc,ckd->qkgd", weights, value_block, preferred_element_type=jnp.float32)
    outputs = mixed.astype(jnp.bfloat16).reshape(block, local_kv * group * HEAD_DIM)
    return outputs


def per_device(tokens, attn_gain, w_query, w_key, w_value, w_out, mlp_gain, w_gate, w_up, w_down):
    rows = tokens.shape[0]
    whole = lax.all_gather(tokens, "tensor", axis=1, tiled=True)
    normed = scaled_rows(whole, attn_gain)
    query_full = lax.all_gather(w_query, "seq", axis=0, tiled=True)
    key_full, value_full = (
        lax.all_gather(w_key, "seq", axis=0, tiled=True),
        lax.all_gather(w_value, "seq", axis=0, tiled=True),
    )
    queries = product(normed, query_full).astype(jnp.bfloat16)
    keys = product(normed, key_full).astype(jnp.bfloat16)
    values = product(normed, value_full).astype(jnp.bfloat16)
    reach = -(-WINDOW // rows)
    earlier = []
    for step in range(reach):
        earlier.append(passed_along((keys, values), "seq", step + 1))
    context_keys = jnp.concatenate(
        [earlier[reach - 1 - step][0] for step in range(reach)] + [keys], axis=0
    )
    context_values = jnp.concatenate(
        [earlier[reach - 1 - step][1] for step in range(reach)] + [values], axis=0
    )
    position = lax.axis_index("seq")
    attended = window_attention(queries, context_keys, context_values, reach, position)
    out_full = lax.all_gather(w_out, "seq", axis=1, tiled=True)
    head_terms = product(attended, out_full)
    share = tokens.shape[1]
    attn_whole = lax.psum(head_terms.astype(jnp.bfloat16), "tensor").astype(jnp.float32)
    stream_whole = (whole.astype(jnp.float32) + attn_whole).astype(jnp.bfloat16)
    stream_share = lax.dynamic_slice_in_dim(
        stream_whole, lax.axis_index("tensor") * share, share, 1
    )
    stream_normed = scaled_rows(stream_whole, mlp_gain)
    gate_full = lax.all_gather(w_gate, "seq", axis=0, tiled=True)
    up_full = lax.all_gather(w_up, "seq", axis=0, tiled=True)
    gate = product(stream_normed, gate_full)
    upward = product(stream_normed, up_full)
    hidden = (jax.nn.silu(gate) * upward).astype(jnp.bfloat16)
    down_full = lax.all_gather(w_down, "seq", axis=1, tiled=True)
    unit_terms = product(hidden, down_full)
    mlp_share = lax.psum_scatter(
        unit_terms.astype(jnp.bfloat16), "tensor", scatter_dimension=1, tiled=True
    ).astype(jnp.float32)
    return (stream_share.astype(jnp.float32) + mlp_share).astype(jnp.bfloat16)


def solution(mesh):
    in_specs = (
        P("seq", "tensor"),
        P(),
        P("seq", "tensor"),
        P("seq", "tensor"),
        P("seq", "tensor"),
        P("tensor", "seq"),
        P(),
        P("seq", "tensor"),
        P("seq", "tensor"),
        P("tensor", "seq"),
    )
    out_specs = P("seq", "tensor")
    return jax.shard_map(
        per_device, mesh=mesh, in_specs=in_specs, out_specs=out_specs, check_vma=False
    )
```

profile of v0, /device:TPU:0, one launch (start us, length us, event | category | flops | bytes accessed | tf_op | source)
XLA Modules:
  0.0 529.0 jit_solution(15447656682437301794)
XLA Ops:
  8.8 33.4 %all_gather.26 = bf16[2048,128]{1,0:T(8,128)(2,1)S(1)} all-gather(bf16[256,128]{1,0:T(8,128)(2,1)} %param.13), channel_id=1, replica_groups=mesh['seq'=8,'tensor'=4] {'seq'}, dimensions={0}, use_global_device_ids=true | all-gather | bytes 589824 | tf_op jit(solution)/shard_map/all_gather | solution.py:61
  42.2 35.2 %all_gather.25 = bf16[2048,128]{1,0:T(8,128)(2,1)} all-gather(bf16[256,128]{1,0:T(8,128)(2,1)} %param.14), channel_id=1, replica_groups=mesh['seq'=8,'tensor'=4] {'seq'}, dimensions={0}, use_global_device_ids=true | all-gather | bytes 589824 | tf_op jit(solution)/shard_map/all_gather | solution.py:62
  77.3 1.3 fusion.14
  78.7 2.2 fusion.7
  80.9 2.4 convolution_convert_fusion.3
  83.3 1.3 collective-permute-start.2
  84.6 4.3 collective-permute-start.3
  89.6 2.7 collective-permute-start
  92.4 2.7 collective-permute-start.1
  95.1 3.0 convolution_convert_fusion.2
  98.1 3.3 fusion.1
  101.4 2.8 fusion
  104.2 4.8 fusion.16
  109.0 33.7 %all-gather.11.cloned.1.call-done = bf16[512,2048]{1,0:T(8,128)(2,1)} async-done(((bf16[512,256]{1,0:T(8,128)(2,1)}), bf16[512,2048]{1,0:T(8,128)(2,1)}) %all-gather.11.cloned.1.call-update) | async-done | bytes 2097168 | tf_op jit(solution)/shard_map/all_gather | solution.py:79
  142.7 4.4 convolution_convert_fusion
  149.3 47.5 %all-reduce.2.cloned.1.call-done = bf16[512,2048]{1,0:T(8,128)(2,1)} async-done(((bf16[512,2048]{1,0:T(8,128)(2,1)}), bf16[512,2048]{1,0:T(8,128)(2,1)}) %all-reduce.2.cloned.1.call-update) | async-done | bytes 2097168 | tf_op jit(solution)/shard_map/psum | solution.py:82
  196.9 3.9 fusion.4
  200.8 90.5 %all-gather.13.cloned.1.call-done = bf16[2048,1408]{1,0:T(8,128)(2,1)} async-done(((bf16[256,1408]{1,0:T(8,128)(2,1)}), bf16[2048,1408]{1,0:T(8,128)(2,1)}) %all-gather.13.cloned.1.call-update) | async-done | bytes 5767184 | tf_op jit(solution)/shard_map/all_gather | solution.py:88
  291.3 8.4 %fusion.21 = f32[512,1408]{1,0:T(8,128)} fusion(bf16[2048,1408]{1,0:T(8,128)(2,1)} %all-gather.13.cloned.1.call-done, bf16[512,2048]{1,0:T(8,128)(2,1)} %get-tuple-element.6, f32[2048]{0:T(1024)S(1)} %copy-done.4, f32[512]{0:T(512)S(1)} %add_rsqrt_fusion), kind=kOutput, calls=%fused_computation.33 | convolution fusion | flops 2956984320 | bytes 10758144 | tf_op jit(solution)/shard_map/dot_general | solution.py:23
  299.7 84.1 %all-gather.15.cloned.1.call-done = bf16[2048,1408]{1,0:T(8,128)(2,1)} async-done(((bf16[256,1408]{1,0:T(8,128)(2,1)}), bf16[2048,1408]{1,0:T(8,128)(2,1)}) %all-gather.15.cloned.1.call-update) | async-done | bytes 5767184 | tf_op jit(solution)/shard_map/all_gather | solution.py:89
  383.9 93.4 %all-gather.17.cloned.1.call-done = bf16[1408,2048]{1,0:T(8,128)(2,1)} async-done(((bf16[1408,256]{1,0:T(8,128)(2,1)}), bf16[1408,2048]{1,0:T(8,128)(2,1)}) %all-gather.17.cloned.1.call-update) | async-done | bytes 5767184 | tf_op jit(solution)/shard_map/all_gather | solution.py:93
  477.2 13.4 %convolution_convert_fusion.1 = bf16[512,2048]{1,0:T(8,128)(2,1)} fusion(bf16[1408,2048]{1,0:T(8,128)(2,1)} %all-gather.17.cloned.1.call-done, bf16[2048,1408]{1,0:T(8,128)(2,1)} %all-gather.15.cloned.1.call-done, f32[512,1408]{1,0:T(8,128)} %fusion.21, bf16[512,2048]{1,0:T(8,128)(2,1)S(1)} %copy-done.1, f32[2048]{0:T(1024)S(1)} %copy-done.4, ...), kind=kOutput, calls=%fused_computation.27 | convolution fusion | flops 5915148288 | bytes 18622464 | tf_op jit(solution)/shard_map/dot_general | solution.py:23
  490.7 29.5 %reduce-scatter.2.cloned.1.call-done = bf16[512,512]{1,0:T(8,128)(2,1)} async-done(((bf16[512,2048]{1,0:T(8,128)(2,1)}), bf16[512,512]{1,0:T(8,128)(2,1)}) %reduce-scatter.2.cloned.1.call-update) | async-done | bytes 524304 | tf_op jit(solution)/shard_map/reduce_scatter | solution.py:95
  520.2 2.0 add_convert_fusion
  (37 shorter events, 5.2 us)
Async XLA Ops:
  6.5 74.4 %copy-start.3 = (f32[2048]{0:T(1024)S(1)}, f32[2048]{0:T(1024)}, u32[]{:S(2)}) copy-start(f32[2048]{0:T(1024)} %param.11) | copy-start | bytes 24580
  6.5 72.1 %all-gather.7.cloned.1.call-start = ((), (), s32[]{:S(2)}) async-start(), calls=%async_computation.1 | async-start | bytes 2621440 | tf_op jit(solution)/shard_map/all_gather | solution.py:57
  7.3 87.8 %all-gather.9.cloned.1.call-start = ((), (), s32[]{:S(2)}) async-start(), calls=%async_computation.2 | async-start | bytes 2359296 | tf_op jit(solution)/shard_map/all_gather | solution.py:59
  8.0 134.7 %all-gather.11.cloned.1.call-start = ((), (), s32[]{:S(2)}) async-start(), calls=%async_computation.3 | async-start | bytes 2359296 | tf_op jit(solution)/shard_map/all_gather | solution.py:79
  8.7 188.1 %all-reduce.2.cloned.1.call-start = ((), (), s32[]{:S(2)}) async-start(), calls=%async_computation.4 | async-start | bytes 4194304 | tf_op jit(solution)/shard_map/psum | solution.py:82
  78.6 10.2 %copy-start = (bf16[512,2048]{1,0:T(8,128)(2,1)S(1)}, bf16[512,2048]{1,0:T(8,128)(2,1)}, u32[]{:S(2)}) copy-start(bf16[512,2048]{1,0:T(8,128)(2,1)} %all-gather.7.cloned.1.call-done) | copy-start | bytes 6291460
  78.7 10.2 %copy-start.2 = (bf16[2048,128]{1,0:T(8,128)(2,1)S(1)}, bf16[2048,128]{1,0:T(8,128)(2,1)}, u32[]{:S(2)}) copy-start(bf16[2048,128]{1,0:T(8,128)(2,1)} %all_gather.25) | copy-start | bytes 1572868
  83.3 14.8 %collective-permute-start.2 = (bf16[512,128]{1,0:T(8,128)(2,1)S(1)}, bf16[512,128]{1,0:T(8,128)(2,1)S(1)}, u32[]{:S(2)}, u32[]{:S(2)}) collective-permute-start(bf16[512,128]{1,0:T(8,128)(2,1)S(1)} %convolution_convert_fusion.3), channel_id=1, source_target_pairs={{0,8},{4,12},{8,16},{12,20},{16,24},{20,28},{1,9},{5,13},{9,17},{1... | collective-permute-start | bytes 393224 | tf_op jit(solution)/shard_map/ppermute | solution.py:13
  84.6 13.5 %collective-permute-start.3 = (bf16[512,128]{1,0:T(8,128)(2,1)S(1)}, bf16[512,128]{1,0:T(8,128)(2,1)}, u32[]{:S(2)}, u32[]{:S(2)}) collective-permute-start(bf16[512,128]{1,0:T(8,128)(2,1)S(1)} %convolution_convert_fusion.3), channel_id=1, source_target_pairs={{0,4},{4,8},{8,12},{12,16},{16,20},{20,24},{24,28},{1,5},{5,9},{9,... | collective-permute-start | bytes 393224 | tf_op jit(solution)/shard_map/ppermute | solution.py:13
  89.6 14.5 %collective-permute-start = (bf16[512,128]{1,0:T(8,128)(2,1)S(1)}, bf16[512,128]{1,0:T(8,128)(2,1)S(1)}, u32[]{:S(2)}, u32[]{:S(2)}) collective-permute-start(bf16[512,128]{1,0:T(8,128)(2,1)S(1)} %convolution_convert_fusion.4), channel_id=1, source_target_pairs={{0,8},{4,12},{8,16},{12,20},{16,24},{20,28},{1,9},{5,13},{9,17},{1... | collective-permute-start | bytes 393224 | tf_op jit(solution)/shard_map/ppermute | solution.py:13
  92.4 11.8 %collective-permute-start.1 = (bf16[512,128]{1,0:T(8,128)(2,1)S(1)}, bf16[512,128]{1,0:T(8,128)(2,1)S(1)}, u32[]{:S(2)}, u32[]{:S(2)}) collective-permute-start(bf16[512,128]{1,0:T(8,128)(2,1)S(1)} %convolution_convert_fusion.4), channel_id=1, source_target_pairs={{0,4},{4,8},{8,12},{12,16},{16,20},{20,24},{24,28},{1,5},{5,9},{9,... | collective-permute-start | bytes 393224 | tf_op jit(solution)/shard_map/ppermute | solution.py:13
  147.1 144.2 %copy-start.4 = (f32[2048]{0:T(1024)S(1)}, f32[2048]{0:T(1024)}, u32[]{:S(2)}) copy-start(f32[2048]{0:T(1024)} %param.16) | copy-start | bytes 24580
  147.1 144.1 %all-gather.13.cloned.1.call-start = ((), (), s32[]{:S(2)}) async-start(), calls=%async_computation.5 | async-start | bytes 6488064 | tf_op jit(solution)/shard_map/all_gather | solution.py:88
  147.7 236.1 %all-gather.15.cloned.1.call-start = ((), (), s32[]{:S(2)}) async-start(), calls=%async_computation.6 | async-start | bytes 6488064 | tf_op jit(solution)/shard_map/all_gather | solution.py:89
  148.3 328.9 %all-gather.17.cloned.1.call-start = ((), (), s32[]{:S(2)}) async-start(), calls=%async_computation.7 | async-start | bytes 6488064 | tf_op jit(solution)/shard_map/all_gather | solution.py:93
  149.1 371.1 %reduce-scatter.2.cloned.1.call-start = ((), (), s32[]{:S(2)}) async-start(), calls=%async_computation.8 | async-start | bytes 2621440 | tf_op jit(solution)/shard_map/reduce_scatter | solution.py:95
  291.3 185.9 %copy-start.1 = (bf16[512,2048]{1,0:T(8,128)(2,1)S(1)}, bf16[512,2048]{1,0:T(8,128)(2,1)}, u32[]{:S(2)}) copy-start(bf16[512,2048]{1,0:T(8,128)(2,1)} %get-tuple-element.6) | copy-start | bytes 6291460
Sparse Core Ops, SparseCore 0:
  8.9 25.2 all-gather.6
  36.3 52.5 all-gather.8
  91.0 51.7 all-gather.10
  147.3 49.5 all-reduce.1
  198.9 92.3 all-gather.12
  293.3 90.4 all-gather.14
  385.9 91.2 all-gather.16
  490.8 29.3 reduce-scatter.1
where the time goes:
time: 529 us
  waiting for transfers between devices  383 us (72%)
  blocking collectives  68.5 us (13%)
  matrix products  40.5 us (8%)
  between operations  13.7 us (3%)
  other arithmetic  12.2 us (2%)
  starting transfers between devices  11.5 us (2%)
    all_gather x1, waiting for transfers between devices, per_device(): down_full = lax.all_gather(w_down, 'seq', axis=1, tiled=True)  93.4 us
    all_gather x1, waiting for transfers between devices, per_device(): gate_full = lax.all_gather(w_gate, 'seq', axis=0, tiled=True)  90.5 us
    all_gather x1, waiting for transfers between devices, per_device(): up_full = lax.all_gather(w_up, 'seq', axis=0, tiled=True)  84.1 us
    psum x1, waiting for transfers between devices, per_device(): lax.psum(head_terms.astype(jnp.bfloat16), 'tensor').astype(jnp.float32)  47.5 us
    all_gather x1, blocking collectives, per_device(): lax.all_gather(w_value, 'seq', axis=0, tiled=True)  35.2 us
    all_gather x1, waiting for transfers between devices, per_device(): out_full = lax.all_gather(w_out, 'seq', axis=1, tiled=True)  33.7 us
    all_gather x1, blocking collectives, per_device(): lax.all_gather(w_key, 'seq', axis=0, tiled=True)  33.4 us
    dot_general x6, matrix products, product(): return jnp.dot(left, right, preferred_element_type=jnp.float32)  32.3 us
  transfers between devices with their start and end apart: 12, of which 6 were waited for; matrix products, arithmetic and copies ran while one was open for 6% of the time, Pallas kernels for 0%

commit v1 on v0

--- a/solution.py
+++ b/solution.py
@@ -53,6 +53,18 @@
 
 
 def per_device(tokens, attn_gain, w_query, w_key, w_value, w_out, mlp_gain, w_gate, w_up, w_down):
+
+    def press_corner_all(unit):
+        p_count = lax.axis_size("seq")
+        tall = [None] * p_count
+        copies = list(map(lambda num: (num, (num + 1) % p_count), range(p_count)))
+        tall[p_count - 1] = unit
+        for u in range(p_count - 2, -1, -1):
+            tall[u] = lax.ppermute(tall[u + 1], "seq", copies)
+        outer = jnp.concatenate(tall, 1)
+        current_value = jnp.roll(outer, shift=(lax.axis_index("seq") + 1) * unit.shape[1], axis=1)
+        return current_value
+
     rows = tokens.shape[0]
     whole = lax.all_gather(tokens, "tensor", axis=1, tiled=True)
     normed = scaled_rows(whole, attn_gain)
@@ -90,7 +102,7 @@
     gate = product(stream_normed, gate_full)
     upward = product(stream_normed, up_full)
     hidden = (jax.nn.silu(gate) * upward).astype(jnp.bfloat16)
-    down_full = lax.all_gather(w_down, "seq", axis=1, tiled=True)
+    down_full = press_corner_all(w_down)
     unit_terms = product(hidden, down_full)
     mlp_share = lax.psum_scatter(
         unit_terms.astype(jnp.bfloat16), "tensor", scatter_dimension=1, tiled=True

time: 529 us -> 485 us (0.917)
  waiting for transfers between devices: 383 us -> 314 us
  local copies, waits for them, and re-layouts: 0.02 us -> 23.6 us
    ppermute x0 -> x7, waiting for transfers between devices: none -> 177 us  [press_corner_all(): tall[u] = lax.ppermute(tall[u + 1], 'seq', copies)]
    all_gather x1 -> x0, waiting for transfers between devices: 93.4 us -> none  [per_device(): down_full = lax.all_gather(w_down, 'seq', axis=1, tiled=True)]
    all_gather x1, waiting for transfers between devices: 90.5 us -> 0.01 us  [per_device(): gate_full = lax.all_gather(w_gate, 'seq', axis=0, tiled=True)]
    psum x1, waiting for transfers between devices: 47.5 us -> 0.01 us  [per_device(): lax.psum(head_terms.astype(jnp.bfloat16), 'tensor').astype(jnp.float32)]
    unnamed x10 -> x43, local copies, waits for them, and re-layouts: 0.02 us -> 22.7 us
    all_gather x1, waiting for transfers between devices: 84.1 us -> 70.8 us  [per_device(): up_full = lax.all_gather(w_up, 'seq', axis=0, tiled=True)]
  transfers between devices with their start and end apart: 12 -> 18, of which waited for: 6 -> 10; matrix products, arithmetic and copies ran while one was open for 6% -> 11% of each run, Pallas kernels for 0% -> 0%
where the time goes in v1:
time: 485 us
  waiting for transfers between devices  314 us (65%)
  blocking collectives  68.5 us (14%)
  matrix products  39.7 us (8%)
  local copies, waits for them, and re-layouts  23.6 us (5%)
  between operations  13.7 us (3%)
  starting transfers between devices  12.7 us (3%)
  other arithmetic  12.3 us (3%)
    ppermute x7, waiting for transfers between devices, press_corner_all(): tall[u] = lax.ppermute(tall[u + 1], 'seq', copies)  177 us
    all_gather x1, waiting for transfers between devices, per_device(): up_full = lax.all_gather(w_up, 'seq', axis=0, tiled=True)  70.8 us
    all_gather x1, blocking collectives, per_device(): lax.all_gather(w_value, 'seq', axis=0, tiled=True)  35.2 us
    all_gather x1, waiting for transfers between devices, per_device(): out_full = lax.all_gather(w_out, 'seq', axis=1, tiled=True)  33.7 us
    all_gather x1, blocking collectives, per_device(): lax.all_gather(w_key, 'seq', axis=0, tiled=True)  33.4 us
    dot_general x6, matrix products, product(): return jnp.dot(left, right, preferred_element_type=jnp.float32)  31.6 us
    reduce_scatter x1, waiting for transfers between devices, per_device(): lax.psum_scatter(unit_terms.astype(jnp.bfloat16), 'tensor', scatter_dimen...  29.5 us
    unnamed x43, local copies, waits for them, and re-layouts  22.7 us
  transfers between devices with their start and end apart: 18, of which 10 were waited for; matrix products, arithmetic and copies ran while one was open for 11% of the time, Pallas kernels for 0%

profile of v1, /device:TPU:0, one launch (start us, length us, event | category | flops | bytes accessed | tf_op | source)
XLA Modules:
  0.0 484.6 jit_solution(8302049509703774637)
XLA Ops:
  8.8 33.4 %all_gather.23 = bf16[2048,128]{1,0:T(8,128)(2,1)S(1)} all-gather(bf16[256,128]{1,0:T(8,128)(2,1)} %param.13), channel_id=1, replica_groups=mesh['seq'=8,'tensor'=4] {'seq'}, dimensions={0}, use_global_device_ids=true | all-gather | bytes 589824 | tf_op jit(solution)/shard_map/all_gather | solution.py:73
  42.2 35.2 %all_gather.22 = bf16[2048,128]{1,0:T(8,128)(2,1)} all-gather(bf16[256,128]{1,0:T(8,128)(2,1)} %param.14), channel_id=1, replica_groups=mesh['seq'=8,'tensor'=4] {'seq'}, dimensions={0}, use_global_device_ids=true | all-gather | bytes 589824 | tf_op jit(solution)/shard_map/all_gather | solution.py:74
  80.9 2.4 convolution_convert_fusion.2
  84.6 4.3 collective-permute-start.3
  89.6 2.7 collective-permute-start
  92.4 2.7 collective-permute-start.1
  95.1 3.0 convolution_convert_fusion.1
  98.1 3.3 fusion.1
  101.4 2.8 fusion
  104.2 4.8 fusion.21
  109.0 33.7 %all-gather.10.cloned.1.call-done = bf16[512,2048]{1,0:T(8,128)(2,1)} async-done(((bf16[512,256]{1,0:T(8,128)(2,1)}), bf16[512,2048]{1,0:T(8,128)(2,1)}) %all-gather.10.cloned.1.call-update) | async-done | bytes 2097168 | tf_op jit(solution)/shard_map/all_gather | solution.py:91
  142.7 4.4 convolution_convert_fusion
  149.9 18.3 %collective-permute-done.4 = bf16[1408,256]{1,0:T(8,128)(2,1)S(1)} collective-permute-done((bf16[1408,256]{1,0:T(8,128)(2,1)S(1)}, bf16[1408,256]{1,0:T(8,128)(2,1)S(1)}, u32[]{:S(2)}, u32[]{:S(2)}) %collective-permute-start.4) | collective-permute-done | bytes 720928 | tf_op jit(solution)/shard_map/ppermute | solution.py:63
  168.2 18.9 %collective-permute-done.5 = bf16[1408,256]{1,0:T(8,128)(2,1)S(1)} collective-permute-done((bf16[1408,256]{1,0:T(8,128)(2,1)S(1)}, bf16[1408,256]{1,0:T(8,128)(2,1)S(1)}, u32[]{:S(2)}, u32[]{:S(2)}) %collective-permute-start.5) | collective-permute-done | bytes 720928 | tf_op jit(solution)/shard_map/ppermute | solution.py:63
  187.9 18.0 %collective-permute-done.6 = bf16[1408,256]{1,0:T(8,128)(2,1)S(1)} collective-permute-done((bf16[1408,256]{1,0:T(8,128)(2,1)S(1)}, bf16[1408,256]{1,0:T(8,128)(2,1)S(1)}, u32[]{:S(2)}, u32[]{:S(2)}) %collective-permute-start.6) | collective-permute-done | bytes 720928 | tf_op jit(solution)/shard_map/ppermute | solution.py:63
  206.8 35.0 %collective-permute-done.7 = bf16[1408,256]{1,0:T(8,128)(2,1)S(1)} collective-permute-done((bf16[1408,256]{1,0:T(8,128)(2,1)S(1)}, bf16[1408,256]{1,0:T(8,128)(2,1)S(1)}, u32[]{:S(2)}, u32[]{:S(2)}) %collective-permute-start.7) | collective-permute-done | bytes 720928 | tf_op jit(solution)/shard_map/ppermute | solution.py:63
  242.7 20.0 %collective-permute-done.8 = bf16[1408,256]{1,0:T(8,128)(2,1)S(1)} collective-permute-done((bf16[1408,256]{1,0:T(8,128)(2,1)S(1)}, bf16[1408,256]{1,0:T(8,128)(2,1)S(1)}, u32[]{:S(2)}, u32[]{:S(2)}) %collective-permute-start.8) | collective-permute-done | bytes 720928 | tf_op jit(solution)/shard_map/ppermute | solution.py:63
  263.6 35.4 %collective-permute-done.9 = bf16[1408,256]{1,0:T(8,128)(2,1)} collective-permute-done((bf16[1408,256]{1,0:T(8,128)(2,1)S(1)}, bf16[1408,256]{1,0:T(8,128)(2,1)}, u32[]{:S(2)}, u32[]{:S(2)}) %collective-permute-start.9) | collective-permute-done | bytes 720928 | tf_op jit(solution)/shard_map/ppermute | solution.py:63
  299.0 4.1 fusion.6
  303.1 31.2 %collective-permute-done.10 = bf16[1408,256]{1,0:T(8,128)(2,1)} collective-permute-done((bf16[1408,256]{1,0:T(8,128)(2,1)}, bf16[1408,256]{1,0:T(8,128)(2,1)}, u32[]{:S(2)}, u32[]{:S(2)}) %collective-permute-start.10) | collective-permute-done | bytes 720928 | tf_op jit(solution)/shard_map/ppermute | solution.py:63
  354.4 7.7 %fusion.26 = f32[512,1408]{1,0:T(8,128)} fusion(bf16[2048,1408]{1,0:T(8,128)(2,1)} %all-gather.12.cloned.1.call-done, bf16[512,2048]{1,0:T(8,128)(2,1)S(1)} %copy-done.1, f32[2048]{0:T(1024)S(1)} %copy-done.13, f32[512]{0:T(512)S(1)} %add_rsqrt_fusion), kind=kOutput, calls=%fused_computation.35 | convolution fusion | flops 2956984320 | bytes 10758144 | tf_op jit(solution)/shard_map/dot_general | solution.py:23
  362.2 70.8 %all-gather.14.cloned.1.call-done = bf16[2048,1408]{1,0:T(8,128)(2,1)} async-done(((bf16[256,1408]{1,0:T(8,128)(2,1)}), bf16[2048,1408]{1,0:T(8,128)(2,1)}) %all-gather.14.cloned.1.call-update) | async-done | bytes 5767184 | tf_op jit(solution)/shard_map/all_gather | solution.py:101
  433.0 13.3 %fusion.18 = bf16[512,2048]{1,0:T(8,128)(2,1)} fusion(bf16[1408,4096]{1,0:T(8,128)(2,1)} %constant_dynamic-update-slice_fusion, s32[]{:T(128)S(6)} %select_n.23, bf16[2048,1408]{1,0:T(8,128)(2,1)} %all-gather.14.cloned.1.call-done, f32[512,1408]{1,0:T(8,128)} %fusion.26, bf16[512,2048]{1,0:T(8,128)(2,1)S(1)} %copy-done.1, f32[2048]{0:T(1024)S(1)} %copy-done.13, ...), kind=kOutput, calls=%fused_computation.28 | convolution fusion | flops 5915148288 | bytes 18622468 | tf_op jit(solution)/shard_map/dot_general | solution.py:23
  446.3 29.5 %reduce-scatter.2.cloned.1.call-done = bf16[512,512]{1,0:T(8,128)(2,1)} async-done(((bf16[512,2048]{1,0:T(8,128)(2,1)}), bf16[512,512]{1,0:T(8,128)(2,1)}) %reduce-scatter.2.cloned.1.call-update) | async-done | bytes 524304 | tf_op jit(solution)/shard_map/reduce_scatter | solution.py:107
  (82 shorter events, 36.2 us)
Async XLA Ops:
  6.5 74.4 %copy-start.12 = (f32[2048]{0:T(1024)S(1)}, f32[2048]{0:T(1024)}, u32[]{:S(2)}) copy-start(f32[2048]{0:T(1024)} %param.11) | copy-start | bytes 24580
  6.5 72.1 %all-gather.6.cloned.1.call-start = ((), (), s32[]{:S(2)}) async-start(), calls=%async_computation.1 | async-start | bytes 2621440 | tf_op jit(solution)/shard_map/all_gather | solution.py:69
  7.3 87.8 %all-gather.8.cloned.1.call-start = ((), (), s32[]{:S(2)}) async-start(), calls=%async_computation.2 | async-start | bytes 2359296 | tf_op jit(solution)/shard_map/all_gather | solution.py:71
  8.0 134.7 %all-gather.10.cloned.1.call-start = ((), (), s32[]{:S(2)}) async-start(), calls=%async_computation.3 | async-start | bytes 2359296 | tf_op jit(solution)/shard_map/all_gather | solution.py:91
  8.7 290.2 %all-reduce.2.cloned.1.call-start = ((), (), s32[]{:S(2)}) async-start(), calls=%async_computation.4 | async-start | bytes 4194304 | tf_op jit(solution)/shard_map/psum | solution.py:94
  78.6 10.2 %copy-start = (bf16[512,2048]{1,0:T(8,128)(2,1)S(1)}, bf16[512,2048]{1,0:T(8,128)(2,1)}, u32[]{:S(2)}) copy-start(bf16[512,2048]{1,0:T(8,128)(2,1)} %all-gather.6.cloned.1.call-done) | copy-start | bytes 6291460
  83.3 14.8 %collective-permute-start.2 = (bf16[512,128]{1,0:T(8,128)(2,1)S(1)}, bf16[512,128]{1,0:T(8,128)(2,1)S(1)}, u32[]{:S(2)}, u32[]{:S(2)}) collective-permute-start(bf16[512,128]{1,0:T(8,128)(2,1)S(1)} %convolution_convert_fusion.2), channel_id=1, source_target_pairs={{0,8},{4,12},{8,16},{12,20},{16,24},{20,28},{1,9},{5,13},{9,17},{1... | collective-permute-start | bytes 393224 | tf_op jit(solution)/shard_map/ppermute | solution.py:13
  84.6 13.5 %collective-permute-start.3 = (bf16[512,128]{1,0:T(8,128)(2,1)S(1)}, bf16[512,128]{1,0:T(8,128)(2,1)}, u32[]{:S(2)}, u32[]{:S(2)}) collective-permute-start(bf16[512,128]{1,0:T(8,128)(2,1)S(1)} %convolution_convert_fusion.2), channel_id=1, source_target_pairs={{0,4},{4,8},{8,12},{12,16},{16,20},{20,24},{24,28},{1,5},{5,9},{9,... | collective-permute-start | bytes 393224 | tf_op jit(solution)/shard_map/ppermute | solution.py:13
  89.6 14.5 %collective-permute-start = (bf16[512,128]{1,0:T(8,128)(2,1)S(1)}, bf16[512,128]{1,0:T(8,128)(2,1)S(1)}, u32[]{:S(2)}, u32[]{:S(2)}) collective-permute-start(bf16[512,128]{1,0:T(8,128)(2,1)S(1)} %convolution_convert_fusion.3), channel_id=1, source_target_pairs={{0,8},{4,12},{8,16},{12,20},{16,24},{20,28},{1,9},{5,13},{9,17},{1... | collective-permute-start | bytes 393224 | tf_op jit(solution)/shard_map/ppermute | solution.py:13
  92.4 11.8 %collective-permute-start.1 = (bf16[512,128]{1,0:T(8,128)(2,1)S(1)}, bf16[512,128]{1,0:T(8,128)(2,1)S(1)}, u32[]{:S(2)}, u32[]{:S(2)}) collective-permute-start(bf16[512,128]{1,0:T(8,128)(2,1)S(1)} %convolution_convert_fusion.3), channel_id=1, source_target_pairs={{0,4},{4,8},{8,12},{12,16},{16,20},{20,24},{24,28},{1,5},{5,9},{9,... | collective-permute-start | bytes 393224 | tf_op jit(solution)/shard_map/ppermute | solution.py:13
  147.2 207.2 %all-gather.12.cloned.1.call-start = ((), (), s32[]{:S(2)}) async-start(), calls=%async_computation.5 | async-start | bytes 6488064 | tf_op jit(solution)/shard_map/all_gather | solution.py:100
  147.7 285.2 %all-gather.14.cloned.1.call-start = ((), (), s32[]{:S(2)}) async-start(), calls=%async_computation.6 | async-start | bytes 6488064 | tf_op jit(solution)/shard_map/all_gather | solution.py:101
  148.3 327.5 %reduce-scatter.2.cloned.1.call-start = ((), (), s32[]{:S(2)}) async-start(), calls=%async_computation.7 | async-start | bytes 2621440 | tf_op jit(solution)/shard_map/reduce_scatter | solution.py:107
  148.4 19.8 %collective-permute-start.4 = (bf16[1408,256]{1,0:T(8,128)(2,1)S(1)}, bf16[1408,256]{1,0:T(8,128)(2,1)S(1)}, u32[]{:S(2)}, u32[]{:S(2)}) collective-permute-start(bf16[1408,256]{1,0:T(8,128)(2,1)S(1)} %copy-done.2), channel_id=1, source_target_pairs={{0,4},{4,8},{8,12},{12,16},{16,20},{20,24},{24,28},{28,0},{1,5},{5... | collective-permute-start | bytes 2162696 | tf_op jit(solution)/shard_map/ppermute | solution.py:63
  168.2 18.9 %collective-permute-start.5 = (bf16[1408,256]{1,0:T(8,128)(2,1)S(1)}, bf16[1408,256]{1,0:T(8,128)(2,1)S(1)}, u32[]{:S(2)}, u32[]{:S(2)}) collective-permute-start(bf16[1408,256]{1,0:T(8,128)(2,1)S(1)} %collective-permute-done.4), channel_id=1, source_target_pairs={{0,4},{4,8},{8,12},{12,16},{16,20},{20,24},{24,28},{28,0},{1,5},{5... | collective-permute-start | bytes 2162696 | tf_op jit(solution)/shard_map/ppermute | solution.py:63
  187.9 18.0 %collective-permute-start.6 = (bf16[1408,256]{1,0:T(8,128)(2,1)S(1)}, bf16[1408,256]{1,0:T(8,128)(2,1)S(1)}, u32[]{:S(2)}, u32[]{:S(2)}) collective-permute-start(bf16[1408,256]{1,0:T(8,128)(2,1)S(1)} %collective-permute-done.5), channel_id=1, source_target_pairs={{0,4},{4,8},{8,12},{12,16},{16,20},{20,24},{24,28},{28,0},{1,5},{5... | collective-permute-start | bytes 2162696 | tf_op jit(solution)/shard_map/ppermute | solution.py:63
  206.8 35.0 %collective-permute-start.7 = (bf16[1408,256]{1,0:T(8,128)(2,1)S(1)}, bf16[1408,256]{1,0:T(8,128)(2,1)S(1)}, u32[]{:S(2)}, u32[]{:S(2)}) collective-permute-start(bf16[1408,256]{1,0:T(8,128)(2,1)S(1)} %collective-permute-done.6), channel_id=1, source_target_pairs={{0,4},{4,8},{8,12},{12,16},{16,20},{20,24},{24,28},{28,0},{1,5},{5... | collective-permute-start | bytes 2162696 | tf_op jit(solution)/shard_map/ppermute | solution.py:63
  242.7 20.0 %collective-permute-start.8 = (bf16[1408,256]{1,0:T(8,128)(2,1)S(1)}, bf16[1408,256]{1,0:T(8,128)(2,1)S(1)}, u32[]{:S(2)}, u32[]{:S(2)}) collective-permute-start(bf16[1408,256]{1,0:T(8,128)(2,1)S(1)} %collective-permute-done.7), channel_id=1, source_target_pairs={{0,4},{4,8},{8,12},{12,16},{16,20},{20,24},{24,28},{28,0},{1,5},{5... | collective-permute-start | bytes 2162696 | tf_op jit(solution)/shard_map/ppermute | solution.py:63
  263.6 35.4 %collective-permute-start.9 = (bf16[1408,256]{1,0:T(8,128)(2,1)S(1)}, bf16[1408,256]{1,0:T(8,128)(2,1)}, u32[]{:S(2)}, u32[]{:S(2)}) collective-permute-start(bf16[1408,256]{1,0:T(8,128)(2,1)S(1)} %collective-permute-done.8), channel_id=1, source_target_pairs={{0,4},{4,8},{8,12},{12,16},{16,20},{20,24},{24,28},{28,0},{1,5},{5... | collective-permute-start | bytes 2162696 | tf_op jit(solution)/shard_map/ppermute | solution.py:63
  299.0 35.3 %collective-permute-start.10 = (bf16[1408,256]{1,0:T(8,128)(2,1)}, bf16[1408,256]{1,0:T(8,128)(2,1)}, u32[]{:S(2)}, u32[]{:S(2)}) collective-permute-start(bf16[1408,256]{1,0:T(8,128)(2,1)} %collective-permute-done.9), channel_id=1, source_target_pairs={{0,4},{4,8},{8,12},{12,16},{16,20},{20,24},{24,28},{28,0},{1,5},{5... | collective-permute-start | bytes 2162696 | tf_op jit(solution)/shard_map/ppermute | solution.py:63
  299.0 39.5 %copy-start.10 = (bf16[1408,256]{1,0:T(8,128)(2,1)S(1)}, bf16[1408,256]{1,0:T(8,128)(2,1)}, u32[]{:S(2)}) copy-start(bf16[1408,256]{1,0:T(8,128)(2,1)} %copy-done.9) | copy-start | bytes 2162692
  299.0 40.5 %copy-start.8 = (bf16[1408,256]{1,0:T(8,128)(2,1)S(1)}, bf16[1408,256]{1,0:T(8,128)(2,1)}, u32[]{:S(2)}) copy-start(bf16[1408,256]{1,0:T(8,128)(2,1)} %copy-done.7) | copy-start | bytes 2162692
  303.1 37.4 %copy-start.6 = (bf16[1408,256]{1,0:T(8,128)(2,1)S(1)}, bf16[1408,256]{1,0:T(8,128)(2,1)}, u32[]{:S(2)}) copy-start(bf16[1408,256]{1,0:T(8,128)(2,1)} %copy-done.5) | copy-start | bytes 2162692
  303.1 38.4 %copy-start.4 = (bf16[1408,256]{1,0:T(8,128)(2,1)S(1)}, bf16[1408,256]{1,0:T(8,128)(2,1)}, u32[]{:S(2)}) copy-start(bf16[1408,256]{1,0:T(8,128)(2,1)} %copy-done.3) | copy-start | bytes 2162692
  (8 other events, 30.9 us)
Sparse Core Ops, SparseCore 0:
  8.9 25.2 all-gather.5
  36.3 52.5 all-gather.7
  91.0 51.7 all-gather.9
  147.3 49.5 all-reduce.1
  198.9 135.5 all-gather.11
  336.6 96.3 all-gather.13
  446.4 29.3 reduce-scatter.1
